TPU v7x, 32 devices: a whole 2x2x4 slice. The times are simulated.
32 devices in a mesh: blk: 8 (over y, x, core), vec: 4 (over z).
Axes of the slice: x: 2, y: 2, z: 4, core: 2. Of those that a mesh axis runs over, the one named last changes fastest.
Arguments:
- trial: bfloat16 [64, 64, 4096], P('vec', None, 'blk'), may hold values from -0.01171875 to 0.01171875
- coupling: bfloat16 [8, 6, 512, 512], P('blk'), may hold values from -0.09375 to 0.09375
- partners: int32 [8, 6], P('blk'), may hold values from 0 to 7, as said below
- live: int32 [8], P('blk'), may hold values from 1 to 6, as said below
- diag_block: bfloat16 [4096, 512], P('blk'), may hold values from -0.25 to 0.25
- beta_coupling: bfloat16 [64, 64], replicated, may hold values from -0.75 to 0.75
- hdiag: float32 [64, 4096], P(None, 'blk'), may hold values from 0.5 to 4
Outputs:
- correction: bfloat16 [64, 64, 4096], P('vec', None, 'blk')
- subspace: float32 [64, 64], P(None, 'vec')
Inputs may be any that keep to these rules, and one draw needn't show every extreme that they name: `partners`: each row holds 6 different block numbers, none equal to the row's own block. `live`: some block uses all 6 slots in every draw.
All inputs are finite; a program needn't handle non-finite values.
Results may differ from a plain program's by a relative error of at most 0.0012.
Values may be sent and summed in bfloat16 or wider, within the bound.
A program may use at most 128 MiB of HBM per device.

v0:
```python
import jax
import jax.numpy as jnp
from jax import lax
from jax.sharding import PartitionSpec as P


def local(trial, coupling, partners, live, diag_block, beta_coupling, hdiag):
    root_count, beta_count, block_width = trial.shape
    row_count = root_count * beta_count
    contract = (((1,), (1,)), ((), ()))
    blocks = coupling[0]
    partner_ids = partners[0]
    live_count = live[0]
    flat = trial.reshape(row_count, block_width)
    sigma_flat = lax.dot_general(flat, diag_block, contract, preferred_element_type=jnp.float32)
    empty = jnp.zeros((row_count, block_width), jnp.float32)
    running = empty
    segment = lax.all_gather(trial, "blk", axis=2, tiled=True)
    span_width = segment.shape[2]
    seg_flat = segment.reshape(row_count, span_width)
    for member in range(blocks.shape[0]):
        relative = partner_ids[member] * block_width
        inside = (relative >= 0) & (relative + block_width <= span_width) & (member < live_count)
        start = jnp.clip(relative, 0, span_width - block_width)

        def multiply(total, start=start, member=member):
            piece = lax.dynamic_slice_in_dim(seg_flat, start, block_width, 1)
            return total + lax.dot_general(
                piece, blocks[member], contract, preferred_element_type=jnp.float32
            )

        def unchanged(total):
            return total

        running = lax.cond(inside, multiply, unchanged, running)
    trial_float = trial.astype(jnp.float32)
    beta_part = jnp.einsum("bc,kca->kba", beta_coupling, trial, preferred_element_type=jnp.float32)
    sigma = (
        (sigma_flat + running).reshape(root_count, beta_count, block_width)
        + beta_part
        + hdiag[None] * trial_float
    )
    all_roots = lax.all_gather(trial, "vec", axis=0, tiled=True)
    intersection_part = jnp.einsum(
        "kba,lba->kl", all_roots.astype(jnp.float32), sigma, precision=lax.Precision.HIGHEST
    )
    total_cells = beta_count * block_width * lax.axis_size("blk")
    theta_part = jnp.einsum("kba,kba->k", trial_float, sigma, precision=lax.Precision.HIGHEST)
    theta = lax.psum(theta_part, "blk")
    resid = sigma - theta[:, None, None] * trial_float
    gap = theta[:, None, None] - hdiag[None]
    raw = resid * gap / (gap * gap + 0.25)
    squares, subspace = lax.psum((jnp.sum(raw * raw, axis=(1, 2)), intersection_part), "blk")
    msq = squares / total_cells
    correction = (raw * lax.rsqrt(msq + 1e-06)[:, None, None]).astype(jnp.bfloat16)
    return (correction, subspace)


def solution(mesh):
    in_specs = (
        P("vec", None, "blk"),
        P("blk", None, None, None),
        P("blk", None),
        P("blk"),
        P("blk", None),
        P(),
        P(None, "blk"),
    )
    out_specs = (P("vec", None, "blk"), P(None, "vec"))
    return jax.shard_map(local, mesh=mesh, in_specs=in_specs, out_specs=out_specs, check_vma=False)
```

profile of v0, /device:TPU:0, one launch (start us, length us, event | category | flops | bytes accessed | tf_op | source)
XLA Modules:
  0.0 180.9 jit_solution(14991319289623215751)
XLA Ops:
  7.2 0.0 copy-start
  7.2 0.0 copy-start.5
  7.2 0.0 all-gather.3.cloned.1.call-start
  7.2 0.7 all-gather.3.cloned.1.call-update
  7.9 0.0 all-gather.5.cloned.1.call-start
  8.0 2.8 %copy.9 = bf16[16,64,512]{2,0,1:T(8,128)(2,1)} copy(bf16[16,64,512]{2,1,0:T(8,128)(2,1)} %param.19) | data formatting | bytes 2097152 | tf_op args[0]
  10.7 0.0 all-gather.5.cloned.1.call-update
  10.8 0.0 copy-done.5
  10.8 0.7 fusion.36
  16.1 52.4 %all-gather.3.cloned.1.call-done = bf16[16,64,4096]{2,1,0:T(8,128)(2,1)} async-done(((bf16[16,64,512]{2,1,0:T(8,128)(2,1)}), bf16[16,64,4096]{2,1,0:T(8,128)(2,1)}) %all-gather.3.cloned.1.call-update) | async-done | bytes 8388624 | tf_op jit(solution)/shard_map/all_gather | solution.py:18
  68.5 2.2 %conditional.6 = (f32[1024,512]{1,0:T(8,128)S(1)}) conditional(s32[]{:T(128)} %convert_element_type.30, () %tuple.44, (s32[1,1]{1,0:T(1,128)}, bf16[1024,4096]{1,0:T(8,128)(2,1)}, bf16[6,512,512]{2,1,0:T(8,128)(2,1)}, s32[1,1]{1,0:T(1,128)}, s32[1,1]{1,0:T(1,128)}) %tuple.81), branch_computations={%region_0.1_spmd, %region_1.2_spmd} | conditional | flops 536870912 | bytes 3670086 | solution.py:35
  68.5 2.2 %fusion = f32[1024,512]{1,0:T(8,128)S(1)} fusion(bf16[1024,4096]{1,0:T(8,128)(2,1)} %get-tuple-element.73, s32[]{:T(128)S(6)} %select_n.12, bf16[6,512,512]{2,1,0:T(8,128)(2,1)} %get-tuple-element.75), kind=kOutput, calls=%fused_computation | convolution fusion | flops 536870912 | bytes 3670020 | tf_op jit(solution)/shard_map/cond/branch_1_fun/dot_general | solution.py:28
  70.7 2.3 %conditional.7 = (f32[1024,512]{1,0:T(8,128)S(1)}) conditional(s32[]{:T(128)} %convert_element_type.29, f32[1024,512]{1,0:T(8,128)S(1)} %get-tuple-element.135, (s32[1,1]{1,0:T(1,128)}, bf16[1024,4096]{1,0:T(8,128)(2,1)}, bf16[6,512,512]{2,1,0:T(8,128)(2,1)}, f32[1024,512]{1,0:T(8,128)S(1)}, s32[1,1]{1,0:T(1,128)}, /*index=5*/s32[1,1]{1,0:T(1,128)}) %tuple.82), branch_computations={%region_2.3_spmd, %region_3.4_spmd} | conditional | flops 537395200 | bytes 5767238 | solution.py:35
  70.7 2.3 %convolution_add_fusion = f32[1024,512]{1,0:T(8,128)S(1)} fusion(f32[1024,512]{1,0:T(8,128)S(1)} %get-tuple-element.76, bf16[1024,4096]{1,0:T(8,128)(2,1)} %get-tuple-element.77, s32[]{:T(128)S(6)} %select_n.13, bf16[6,512,512]{2,1,0:T(8,128)(2,1)} %get-tuple-element.79), kind=kOutput, calls=%fused_computation.5 | convolution fusion | flops 537395200 | bytes 5767172 | tf_op jit(solution)/shard_map/cond/branch_1_fun/dot_general | solution.py:28
  73.0 2.3 %conditional.8 = (f32[1024,512]{1,0:T(8,128)S(1)}) conditional(s32[]{:T(128)} %convert_element_type.28, f32[1024,512]{1,0:T(8,128)S(1)} %get-tuple-element.136, (s32[1,1]{1,0:T(1,128)}, bf16[1024,4096]{1,0:T(8,128)(2,1)}, bf16[6,512,512]{2,1,0:T(8,128)(2,1)}, f32[1024,512]{1,0:T(8,128)S(1)}, s32[1,1]{1,0:T(1,128)}, /*index=5*/s32[1,1]{1,0:T(1,128)}) %tuple.83), branch_computations={%region_4.5_spmd, %region_5.6_spmd} | conditional | flops 537395200 | bytes 5767238 | solution.py:35
  73.0 2.3 %convolution_add_fusion.1 = f32[1024,512]{1,0:T(8,128)S(1)} fusion(f32[1024,512]{1,0:T(8,128)S(1)} %get-tuple-element.80, bf16[1024,4096]{1,0:T(8,128)(2,1)} %get-tuple-element.81, s32[]{:T(128)S(6)} %select_n.14, bf16[6,512,512]{2,1,0:T(8,128)(2,1)} %get-tuple-element.83), kind=kOutput, calls=%fused_computation.10 | convolution fusion | flops 537395200 | bytes 5767172 | tf_op jit(solution)/shard_map/cond/branch_1_fun/dot_general | solution.py:28
  75.3 2.2 %conditional.9 = (f32[1024,512]{1,0:T(8,128)S(1)}) conditional(s32[]{:T(128)} %convert_element_type.27, f32[1024,512]{1,0:T(8,128)S(1)} %get-tuple-element.137, (s32[1,1]{1,0:T(1,128)}, bf16[1024,4096]{1,0:T(8,128)(2,1)}, bf16[6,512,512]{2,1,0:T(8,128)(2,1)}, f32[1024,512]{1,0:T(8,128)S(1)}, s32[1,1]{1,0:T(1,128)}, /*index=5*/s32[1,1]{1,0:T(1,128)}) %tuple.84), branch_computations={%region_6.7_spmd, %region_7.8_spmd} | conditional | flops 537395200 | bytes 5767238 | solution.py:35
  75.3 2.2 %convolution_add_fusion.2 = f32[1024,512]{1,0:T(8,128)S(1)} fusion(f32[1024,512]{1,0:T(8,128)S(1)} %get-tuple-element.84, bf16[1024,4096]{1,0:T(8,128)(2,1)} %get-tuple-element.85, s32[]{:T(128)S(6)} %select_n.15, bf16[6,512,512]{2,1,0:T(8,128)(2,1)} %get-tuple-element.87), kind=kOutput, calls=%fused_computation.15 | convolution fusion | flops 537395200 | bytes 5767172 | tf_op jit(solution)/shard_map/cond/branch_1_fun/dot_general | solution.py:28
  77.5 2.5 %conditional.10 = (f32[1024,512]{1,0:T(8,128)S(1)}) conditional(s32[]{:T(128)} %convert_element_type.26, f32[1024,512]{1,0:T(8,128)S(1)} %get-tuple-element.138, (s32[1,1]{1,0:T(1,128)}, bf16[1024,4096]{1,0:T(8,128)(2,1)}, bf16[6,512,512]{2,1,0:T(8,128)(2,1)}, f32[1024,512]{1,0:T(8,128)S(1)}, s32[1,1]{1,0:T(1,128)}, ...), branch_computations={%region_8.9_spmd, %region_9.10_spmd} | conditional | flops 537395200 | bytes 5767238 | solution.py:35
  77.5 2.5 %convolution_add_fusion.3 = f32[1024,512]{1,0:T(8,128)S(1)} fusion(f32[1024,512]{1,0:T(8,128)S(1)} %get-tuple-element.88, bf16[1024,4096]{1,0:T(8,128)(2,1)} %get-tuple-element.89, s32[]{:T(128)S(6)} %select_n.16, bf16[6,512,512]{2,1,0:T(8,128)(2,1)} %get-tuple-element.91), kind=kOutput, calls=%fused_computation.20 | convolution fusion | flops 537395200 | bytes 5767172 | tf_op jit(solution)/shard_map/cond/branch_1_fun/dot_general | solution.py:28
  80.0 2.4 %conditional.11 = (f32[1024,512]{1,0:T(8,128)S(1)}) conditional(s32[]{:T(128)} %convert_element_type.25, f32[1024,512]{1,0:T(8,128)S(1)} %get-tuple-element.139, (s32[]{:T(128)}, bf16[1024,4096]{1,0:T(8,128)(2,1)}, bf16[6,512,512]{2,1,0:T(8,128)(2,1)}, f32[1024,512]{1,0:T(8,128)S(1)}) %tuple.86), branch_computations={%region_10.11_spmd, %region_11.12_spmd} | conditional | flops 537395200 | bytes 5767204 | solution.py:35
  80.1 2.4 %convolution_add_fusion.4 = f32[1024,512]{1,0:T(8,128)S(1)} fusion(f32[1024,512]{1,0:T(8,128)S(1)} %get-tuple-element.92, bf16[1024,4096]{1,0:T(8,128)(2,1)} %get-tuple-element.93, s32[]{:T(128)S(6)} %min.24, bf16[6,512,512]{2,1,0:T(8,128)(2,1)} %get-tuple-element.95), kind=kOutput, calls=%fused_computation.25 | convolution fusion | flops 537395200 | bytes 5767172 | tf_op jit(solution)/shard_map/cond/branch_1_fun/dot_general | solution.py:28
  82.5 0.0 copy-done
  82.5 0.0 copy-start.1
  82.5 0.0 copy-start.4
  82.5 0.0 copy-start.6
  82.5 2.0 %convolution_add_fusion.5 = f32[1024,512]{1,0:T(8,128)S(1)} fusion(f32[1024,512]{1,0:T(8,128)S(1)} %get-tuple-element.140, bf16[1024,512]{1,0:T(8,128)(2,1)} %bitcast.60, bf16[512,512]{1,0:T(8,128)(2,1)S(1)} %copy-done), kind=kOutput, calls=%fused_computation.44 | convolution fusion | flops 537395200 | bytes 5767168 | tf_op jit(solution)/shard_map/dot_general | solution.py:15
  84.6 0.0 copy-done.1
  84.6 0.0 copy-done.4
  84.6 0.0 copy-done.6
  84.6 0.0 copy-start.2
  84.6 2.0 %multiply_reduce_fusion = (f32[16]{0:T(128)S(1)}, f32[16,64,512]{2,1,0:T(8,128)}) fusion(bf16[16,64,512]{2,1,0:T(8,128)(2,1)S(1)} %copy-done.1, f32[64,512]{1,0:T(8,128)S(1)} %copy-done.4, f32[16,64,512]{2,1,0:T(8,128)S(1)} %bitcast.61, bf16[64,64]{1,0:T(8,128)(2,1)S(1)} %copy-done.6), kind=kOutput, calls=%fused_computation.39 | convolution fusion | flops 70778864 | bytes 5382208 | tf_op jit(solution)/shard_map/bc,kca->kba/dot_general | solution.py:37
  86.7 12.6 %psum.21 = f32[16]{0:T(128)S(1)} all-reduce(f32[16]{0:T(128)S(1)} %get-tuple-element.133), channel_id=1, replica_groups=mesh['blk'=8,'vec'=4] {'blk'}, use_global_device_ids=true, to_apply=%region_12.13 | all-reduce | flops 16 | bytes 128 | tf_op jit(solution)/shard_map/psum | solution.py:49
  99.3 0.0 copy-done.2
  99.3 3.7 %multiply_reduce_fusion.1 = (f32[16]{0:T(128)S(1)}, f32[16,64,512]{2,1,0:T(8,128)}) fusion(f32[64,512]{1,0:T(8,128)S(1)} %copy-done.4, f32[16,64,512]{2,1,0:T(8,128)} %get-tuple-element.134, bf16[16,64,512]{2,1,0:T(8,128)(2,1)S(1)} %copy-done.2, f32[16]{0:T(128)S(1)} %psum.21), kind=kLoop, calls=%fused_computation.43 | loop fusion | flops 5242864 | bytes 5374080 | tf_op jit(solution)/shard_map/reduce_sum | solution.py:53
  103.0 0.0 copy-start.3
  103.0 48.4 %all-gather.5.cloned.1.call-done = bf16[64,64,512]{2,0,1:T(8,128)(2,1)} async-done(((bf16[16,64,512]{2,0,1:T(8,128)(2,1)}), bf16[64,64,512]{2,0,1:T(8,128)(2,1)}) %all-gather.5.cloned.1.call-update) | async-done | bytes 4194320 | tf_op jit(solution)/shard_map/all_gather | solution.py:43
  151.4 6.8 %fusion.31 = f32[64,16]{0,1:T(8,128)S(1)} fusion(bf16[64,64,512]{2,0,1:T(8,128)(2,1)} %all-gather.5.cloned.1.call-done, f32[16,64,512]{2,1,0:T(8,128)} %get-tuple-element.134), kind=kOutput, calls=%fused_computation.45 | convolution fusion | flops 402653184 | bytes 6295552 | tf_op jit(solution)/shard_map/kba,lba->kl/dot_general | solution.py:44
  158.2 14.6 %all-reduce = (f32[16]{0:T(128)S(1)}, f32[64,16]{0,1:T(8,128)}) all-reduce(f32[16]{0:T(128)S(1)} %get-tuple-element.125, f32[64,16]{0,1:T(8,128)S(1)} %fusion.31), channel_id=1, replica_groups=mesh['blk'=8,'vec'=4] {'blk'}, use_global_device_ids=true, to_apply=%region_14.15 | all-reduce | flops 1040 | bytes 8320 | tf_op jit(solution)/shard_map/psum | solution.py:53
  172.8 0.0 copy-done.3
  172.8 1.3 multiply_convert_fusion
  (1 shorter events, 0.0 us)
Async XLA Ops:
  7.2 75.3 %copy-start = (bf16[512,512]{1,0:T(8,128)(2,1)S(1)}, bf16[512,512]{1,0:T(8,128)(2,1)}, u32[]{:S(2)}) copy-start(bf16[512,512]{1,0:T(8,128)(2,1)} %param.23) | copy-start | bytes 1572868
  7.2 3.6 %copy-start.5 = (s32[1,6]{1,0:T(1,128)S(1)}, s32[1,6]{1,0:T(1,128)}, u32[]{:S(2)}) copy-start(s32[1,6]{1,0:T(1,128)} %param.21) | copy-start | bytes 76
  7.2 61.3 %all-gather.3.cloned.1.call-start = ((), (), s32[]{:S(2)}) async-start(), calls=%async_computation | async-start | bytes 9437184 | tf_op jit(solution)/shard_map/all_gather | solution.py:18
  7.9 143.5 %all-gather.5.cloned.1.call-start = ((), (), s32[]{:S(2)}) async-start(), calls=%async_computation.1 | async-start | bytes 5242880 | tf_op jit(solution)/shard_map/all_gather | solution.py:43
  82.5 2.1 %copy-start.1 = (bf16[16,64,512]{2,1,0:T(8,128)(2,1)S(1)}, bf16[16,64,512]{2,1,0:T(8,128)(2,1)}, u32[]{:S(2)}) copy-start(bf16[16,64,512]{2,1,0:T(8,128)(2,1)} %param.19) | copy-start | bytes 3145732
  82.5 2.1 %copy-start.4 = (f32[64,512]{1,0:T(8,128)S(1)}, f32[64,512]{1,0:T(8,128)}, u32[]{:S(2)}) copy-start(f32[64,512]{1,0:T(8,128)} %param.25) | copy-start | bytes 393220
  82.5 2.1 %copy-start.6 = (bf16[64,64]{1,0:T(8,128)(2,1)S(1)}, bf16[64,64]{1,0:T(8,128)(2,1)}, u32[]{:S(2)}) copy-start(bf16[64,64]{1,0:T(8,128)(2,1)} %param.24) | copy-start | bytes 24580
  84.6 14.6 %copy-start.2 = (bf16[16,64,512]{2,1,0:T(8,128)(2,1)S(1)}, bf16[16,64,512]{2,1,0:T(8,128)(2,1)}, u32[]{:S(2)}) copy-start(bf16[16,64,512]{2,1,0:T(8,128)(2,1)} %param.19) | copy-start | bytes 3145732
  103.0 69.8 %copy-start.3 = (f32[16,64,512]{2,1,0:T(8,128)S(1)}, f32[16,64,512]{2,1,0:T(8,128)}, u32[]{:S(2)}) copy-start(f32[16,64,512]{2,1,0:T(8,128)} %get-tuple-element.126) | copy-start | bytes 6291460
Sparse Core Ops, SparseCore 0:
  9.9 58.5 all-gather.2
  70.6 80.7 all-gather.4
where the time goes:
time: 181 us
  waiting for transfers between devices  102 us (56%)
  blocking collectives  27.1 us (15%)
  matrix products  24.7 us (14%)
  between operations  18.8 us (10%)
  other arithmetic  5.05 us (3%)
  local copies, waits for them, and re-layouts  3.5 us (2%)
    all_gather x1, waiting for transfers between devices, local(): segment = lax.all_gather(trial, 'blk', axis=2, tiled=True)  52.4 us
    all_gather x1, waiting for transfers between devices, local(): all_roots = lax.all_gather(trial, 'vec', axis=0, tiled=True)  48.4 us
    psum x1, blocking collectives, local(): lax.psum((jnp.sum(raw * raw, axis=(1, 2)), intersection_part), 'blk')  14.6 us
    dot_general x6, matrix products, multiply(): lax.dot_general(piece, blocks[member], contract, preferred_element_type=j...  13.8 us
    psum x1, blocking collectives, local(): theta = lax.psum(theta_part, 'blk')  12.6 us
    dot_general x1, matrix products, local(): jnp.einsum('kba,lba->kl', all_roots.astype(jnp.float32), sigma, precision...  6.82 us
    reduce_sum x1, other arithmetic, local(): jnp.sum(raw * raw, axis=(1, 2))  3.74 us
  transfers between devices with their start and end apart: 2, of which 2 were waited for; matrix products, arithmetic and copies ran while one was open for 14% of the time, Pallas kernels for 0%

commit v1 on v0

--- a/solution.py
+++ b/solution.py
@@ -40,7 +40,12 @@
         + beta_part
         + hdiag[None] * trial_float
     )
-    all_roots = lax.all_gather(trial, "vec", axis=0, tiled=True)
+    ring = [trial]
+    for hop in range(3):
+        ring.append(lax.ppermute(ring[-1], "vec", [(dev, (dev + 1) % 4) for dev in range(4)]))
+    all_roots = jnp.roll(
+        jnp.concatenate(ring[::-1], axis=0), (lax.axis_index("vec") + 1) * ring[0].shape[0], axis=0
+    )
     intersection_part = jnp.einsum(
         "kba,lba->kl", all_roots.astype(jnp.float32), sigma, precision=lax.Precision.HIGHEST
     )

time: 181 us -> 163 us (0.901)
  waiting for transfers between devices: 102 us -> 72.1 us
  local copies, waits for them, and re-layouts: 3.5 us -> 14.7 us
  starting transfers between devices: 0.08 us -> 3.15 us
  blocking collectives: 27.1 us -> 24.6 us
    ppermute x0 -> x3, waiting for transfers between devices: none -> 71.4 us  [local(): lax.ppermute(ring[-1], 'vec', [(dev, (dev + 1) % 4) for dev in range(4)])]
    all_gather x1, waiting for transfers between devices: 52.4 us -> 0.01 us  [local(): segment = lax.all_gather(trial, 'blk', axis=2, tiled=True)]
    all_gather x1 -> x0, waiting for transfers between devices: 48.4 us -> none  [local(): all_roots = lax.all_gather(trial, 'vec', axis=0, tiled=True)]
    unnamed x15 -> x26, local copies, waits for them, and re-layouts: 2.82 us -> 12.4 us
    ppermute x0 -> x3, starting transfers between devices: none -> 3.11 us  [local(): lax.ppermute(ring[-1], 'vec', [(dev, (dev + 1) % 4) for dev in range(4)])]
  transfers between devices with their start and end apart: 2 -> 4, of which waited for: 2 -> 3; matrix products, arithmetic and copies ran while one was open for 14% -> 9% of each run, Pallas kernels for 0% -> 0%
where the time goes in v1:
time: 163 us; the launch traced here: 162 us
  waiting for transfers between devices  72.1 us (44%)
  blocking collectives  24.6 us (15%)
  matrix products  23.4 us (14%)
  between operations  18.8 us (12%)
  local copies, waits for them, and re-layouts  14.7 us (9%)
  other arithmetic  5.22 us (3%)
  starting transfers between devices  3.15 us (2%)
    ppermute x3, waiting for transfers between devices, local(): lax.ppermute(ring[-1], 'vec', [(dev, (dev + 1) % 4) for dev in range(4)])  71.4 us
    dot_general x6, matrix products, multiply(): lax.dot_general(piece, blocks[member], contract, preferred_element_type=j...  13.5 us
    psum x1, blocking collectives, local(): lax.psum((jnp.sum(raw * raw, axis=(1, 2)), intersection_part), 'blk')  12.9 us
    unnamed x26, local copies, waits for them, and re-layouts  12.4 us
    psum x1, blocking collectives, local(): theta = lax.psum(theta_part, 'blk')  11.8 us
    dot_general x1, matrix products, local(): jnp.einsum('kba,lba->kl', all_roots.astype(jnp.float32), sigma, precision...  5.87 us
    reduce_sum x1, other arithmetic, local(): jnp.sum(raw * raw, axis=(1, 2))  3.91 us
  transfers between devices with their start and end apart: 4, of which 3 were waited for; matrix products, arithmetic and copies ran while one was open for 9% of the time, Pallas kernels for 0%

profile of v1, /device:TPU:0, one launch (start us, length us, event | category | flops | bytes accessed | tf_op | source)
XLA Modules:
  0.0 162.1 jit_solution(13304057525783974036)
XLA Ops:
  7.2 0.0 copy-start
  7.2 0.0 copy-start.7
  7.2 0.0 all-gather.2.cloned.1.call-start
  7.2 0.7 all-gather.2.cloned.1.call-update
  7.9 1.8 %copy.9 = bf16[16,64,512]{2,0,1:T(8,128)(2,1)S(1)} copy(bf16[16,64,512]{2,1,0:T(8,128)(2,1)} %param.19) | data formatting | bytes 2097152 | tf_op args[0]
  9.7 3.1 %collective-permute-start = (bf16[16,64,512]{2,0,1:T(8,128)(2,1)S(1)}, bf16[16,64,512]{2,0,1:T(8,128)(2,1)S(1)}, u32[]{:S(2)}, u32[]{:S(2)}) collective-permute-start(bf16[16,64,512]{2,0,1:T(8,128)(2,1)S(1)} %copy.9), channel_id=1, source_target_pairs={{0,1},{1,2},{2,3},{3,0},{4,5},{5,6},{6,7},{7,4},{8,9},{9,10},{10,1... | collective-permute-start | bytes 3145736 | tf_op jit(solution)/shard_map/ppermute | solution.py:45
  12.8 25.2 %collective-permute-done = bf16[16,64,512]{2,0,1:T(8,128)(2,1)S(1)} collective-permute-done((bf16[16,64,512]{2,0,1:T(8,128)(2,1)S(1)}, bf16[16,64,512]{2,0,1:T(8,128)(2,1)S(1)}, u32[]{:S(2)}, u32[]{:S(2)}) %collective-permute-start) | collective-permute-done | bytes 1048608 | tf_op jit(solution)/shard_map/ppermute | solution.py:45
  38.0 0.0 collective-permute-start.1
  38.0 26.1 %collective-permute-done.1 = bf16[16,64,512]{2,0,1:T(8,128)(2,1)S(1)} collective-permute-done((bf16[16,64,512]{2,0,1:T(8,128)(2,1)S(1)}, bf16[16,64,512]{2,0,1:T(8,128)(2,1)S(1)}, u32[]{:S(2)}, u32[]{:S(2)}) %collective-permute-start.1) | collective-permute-done | bytes 1048608 | tf_op jit(solution)/shard_map/ppermute | solution.py:45
  64.1 0.0 collective-permute-start.2
  64.1 0.0 copy-done.7
  64.1 0.7 fusion.40
  69.4 20.1 %collective-permute-done.2 = bf16[16,64,512]{2,0,1:T(8,128)(2,1)} collective-permute-done((bf16[16,64,512]{2,0,1:T(8,128)(2,1)S(1)}, bf16[16,64,512]{2,0,1:T(8,128)(2,1)}, u32[]{:S(2)}, u32[]{:S(2)}) %collective-permute-start.2) | collective-permute-done | bytes 1048608 | tf_op jit(solution)/shard_map/ppermute | solution.py:45
  89.5 2.3 %constant_dynamic-update-slice_fusion.7 = bf16[128,64,512]{2,0,1:T(8,128)(2,1)} fusion(bf16[16,64,512]{2,0,1:T(8,128)(2,1)} %collective-permute-done.2), kind=kLoop, calls=%fused_computation.54 | loop fusion | bytes 2097152
  91.8 1.1 constant_dynamic-update-slice_fusion.6
  92.9 1.1 constant_dynamic-update-slice_fusion.5
  94.0 0.0 copy-done.1
  94.0 1.6 constant_dynamic-update-slice_fusion.4
  95.6 2.3 %constant_dynamic-update-slice_fusion.3 = bf16[128,64,512]{2,0,1:T(8,128)(2,1)} fusion(bf16[128,64,512]{2,0,1:T(8,128)(2,1)} %constant_dynamic-update-slice_fusion.4, bf16[16,64,512]{2,0,1:T(8,128)(2,1)} %collective-permute-done.2), kind=kLoop, calls=%fused_computation.50 | loop fusion | bytes 2097152
  97.9 1.1 constant_dynamic-update-slice_fusion.2
  99.0 1.1 constant_dynamic-update-slice_fusion.1
  100.1 1.6 constant_dynamic-update-slice_fusion
  101.7 2.2 %conditional.6 = (f32[1024,512]{1,0:T(8,128)S(1)}) conditional(s32[]{:T(128)} %convert_element_type.30, () %tuple.44, (s32[1,1]{1,0:T(1,128)}, bf16[1024,4096]{1,0:T(8,128)(2,1)}, bf16[6,512,512]{2,1,0:T(8,128)(2,1)}, s32[1,1]{1,0:T(1,128)}, s32[1,1]{1,0:T(1,128)}) %tuple.79), branch_computations={%region_0.1_spmd, %region_1.2_spmd} | conditional | flops 536870912 | bytes 3670086 | solution.py:35
  101.7 2.2 %fusion = f32[1024,512]{1,0:T(8,128)S(1)} fusion(bf16[1024,4096]{1,0:T(8,128)(2,1)} %get-tuple-element.73, s32[]{:T(128)S(6)} %select_n.23, bf16[6,512,512]{2,1,0:T(8,128)(2,1)} %get-tuple-element.75), kind=kOutput, calls=%fused_computation | convolution fusion | flops 536870912 | bytes 3670020 | tf_op jit(solution)/shard_map/cond/branch_1_fun/dot_general | solution.py:28
  103.9 2.3 %conditional.7 = (f32[1024,512]{1,0:T(8,128)S(1)}) conditional(s32[]{:T(128)} %convert_element_type.29, f32[1024,512]{1,0:T(8,128)S(1)} %get-tuple-element.135, (s32[1,1]{1,0:T(1,128)}, bf16[1024,4096]{1,0:T(8,128)(2,1)}, bf16[6,512,512]{2,1,0:T(8,128)(2,1)}, f32[1024,512]{1,0:T(8,128)S(1)}, s32[1,1]{1,0:T(1,128)}, /*index=5*/s32[1,1]{1,0:T(1,128)}) %tuple.80), branch_computations={%region_2.3_spmd, %region_3.4_spmd} | conditional | flops 537395200 | bytes 5767238 | solution.py:35
  103.9 2.3 %convolution_add_fusion = f32[1024,512]{1,0:T(8,128)S(1)} fusion(f32[1024,512]{1,0:T(8,128)S(1)} %get-tuple-element.76, bf16[1024,4096]{1,0:T(8,128)(2,1)} %get-tuple-element.77, s32[]{:T(128)S(6)} %select_n.24, bf16[6,512,512]{2,1,0:T(8,128)(2,1)} %get-tuple-element.79), kind=kOutput, calls=%fused_computation.5 | convolution fusion | flops 537395200 | bytes 5767172 | tf_op jit(solution)/shard_map/cond/branch_1_fun/dot_general | solution.py:28
  106.2 2.3 %conditional.8 = (f32[1024,512]{1,0:T(8,128)S(1)}) conditional(s32[]{:T(128)} %convert_element_type.28, f32[1024,512]{1,0:T(8,128)S(1)} %get-tuple-element.136, (s32[1,1]{1,0:T(1,128)}, bf16[1024,4096]{1,0:T(8,128)(2,1)}, bf16[6,512,512]{2,1,0:T(8,128)(2,1)}, f32[1024,512]{1,0:T(8,128)S(1)}, s32[1,1]{1,0:T(1,128)}, /*index=5*/s32[1,1]{1,0:T(1,128)}) %tuple.81), branch_computations={%region_4.5_spmd, %region_5.6_spmd} | conditional | flops 537395200 | bytes 5767238 | solution.py:35
  106.2 2.3 %convolution_add_fusion.1 = f32[1024,512]{1,0:T(8,128)S(1)} fusion(f32[1024,512]{1,0:T(8,128)S(1)} %get-tuple-element.80, bf16[1024,4096]{1,0:T(8,128)(2,1)} %get-tuple-element.81, s32[]{:T(128)S(6)} %select_n.25, bf16[6,512,512]{2,1,0:T(8,128)(2,1)} %get-tuple-element.83), kind=kOutput, calls=%fused_computation.10 | convolution fusion | flops 537395200 | bytes 5767172 | tf_op jit(solution)/shard_map/cond/branch_1_fun/dot_general | solution.py:28
  108.5 2.2 %conditional.9 = (f32[1024,512]{1,0:T(8,128)S(1)}) conditional(s32[]{:T(128)} %convert_element_type.27, f32[1024,512]{1,0:T(8,128)S(1)} %get-tuple-element.137, (s32[1,1]{1,0:T(1,128)}, bf16[1024,4096]{1,0:T(8,128)(2,1)}, bf16[6,512,512]{2,1,0:T(8,128)(2,1)}, f32[1024,512]{1,0:T(8,128)S(1)}, s32[1,1]{1,0:T(1,128)}, /*index=5*/s32[1,1]{1,0:T(1,128)}) %tuple.82), branch_computations={%region_6.7_spmd, %region_7.8_spmd} | conditional | flops 537395200 | bytes 5767238 | solution.py:35
  108.5 2.2 %convolution_add_fusion.2 = f32[1024,512]{1,0:T(8,128)S(1)} fusion(f32[1024,512]{1,0:T(8,128)S(1)} %get-tuple-element.84, bf16[1024,4096]{1,0:T(8,128)(2,1)} %get-tuple-element.85, s32[]{:T(128)S(6)} %select_n.26, bf16[6,512,512]{2,1,0:T(8,128)(2,1)} %get-tuple-element.87), kind=kOutput, calls=%fused_computation.15 | convolution fusion | flops 537395200 | bytes 5767172 | tf_op jit(solution)/shard_map/cond/branch_1_fun/dot_general | solution.py:28
  110.7 2.3 %conditional.10 = (f32[1024,512]{1,0:T(8,128)S(1)}) conditional(s32[]{:T(128)} %convert_element_type.26, f32[1024,512]{1,0:T(8,128)S(1)} %get-tuple-element.138, (s32[1,1]{1,0:T(1,128)}, bf16[1024,4096]{1,0:T(8,128)(2,1)}, bf16[6,512,512]{2,1,0:T(8,128)(2,1)}, f32[1024,512]{1,0:T(8,128)S(1)}, s32[1,1]{1,0:T(1,128)}, ...), branch_computations={%region_8.9_spmd, %region_9.10_spmd} | conditional | flops 537395200 | bytes 5767238 | solution.py:35
  110.7 2.3 %convolution_add_fusion.3 = f32[1024,512]{1,0:T(8,128)S(1)} fusion(f32[1024,512]{1,0:T(8,128)S(1)} %get-tuple-element.88, bf16[1024,4096]{1,0:T(8,128)(2,1)} %get-tuple-element.89, s32[]{:T(128)S(6)} %select_n.27, bf16[6,512,512]{2,1,0:T(8,128)(2,1)} %get-tuple-element.91), kind=kOutput, calls=%fused_computation.20 | convolution fusion | flops 537395200 | bytes 5767172 | tf_op jit(solution)/shard_map/cond/branch_1_fun/dot_general | solution.py:28
  113.0 2.3 %conditional.11 = (f32[1024,512]{1,0:T(8,128)S(1)}) conditional(s32[]{:T(128)} %convert_element_type.25, f32[1024,512]{1,0:T(8,128)S(1)} %get-tuple-element.139, (s32[]{:T(128)}, bf16[1024,4096]{1,0:T(8,128)(2,1)}, bf16[6,512,512]{2,1,0:T(8,128)(2,1)}, f32[1024,512]{1,0:T(8,128)S(1)}) %tuple.84), branch_computations={%region_10.11_spmd, %region_11.12_spmd} | conditional | flops 537395200 | bytes 5767204 | solution.py:35
  113.0 2.3 %convolution_add_fusion.4 = f32[1024,512]{1,0:T(8,128)S(1)} fusion(f32[1024,512]{1,0:T(8,128)S(1)} %get-tuple-element.92, bf16[1024,4096]{1,0:T(8,128)(2,1)} %get-tuple-element.93, s32[]{:T(128)S(6)} %min.24, bf16[6,512,512]{2,1,0:T(8,128)(2,1)} %get-tuple-element.95), kind=kOutput, calls=%fused_computation.25 | convolution fusion | flops 537395200 | bytes 5767172 | tf_op jit(solution)/shard_map/cond/branch_1_fun/dot_general | solution.py:28
  115.3 0.0 copy-done
  115.3 0.0 copy-start.2
  115.3 0.0 copy-start.6
  115.3 0.0 copy-start.8
  115.4 2.1 %convolution_add_fusion.5 = f32[1024,512]{1,0:T(8,128)S(1)} fusion(f32[1024,512]{1,0:T(8,128)S(1)} %get-tuple-element.140, bf16[1024,512]{1,0:T(8,128)(2,1)} %bitcast.57, bf16[512,512]{1,0:T(8,128)(2,1)S(1)} %copy-done), kind=kOutput, calls=%fused_computation.45 | convolution fusion | flops 537395200 | bytes 5767168 | tf_op jit(solution)/shard_map/dot_general | solution.py:15
  117.4 0.0 copy-start.3
  117.5 2.0 %multiply_reduce_fusion = (f32[16]{0:T(128)S(1)}, f32[16,64,512]{2,1,0:T(8,128)}) fusion(bf16[16,64,512]{2,1,0:T(8,128)(2,1)S(1)} %copy-done.2, f32[64,512]{1,0:T(8,128)S(1)} %copy-done.6, f32[16,64,512]{2,1,0:T(8,128)S(1)} %bitcast.58, bf16[64,64]{1,0:T(8,128)(2,1)S(1)} %copy-done.8), kind=kOutput, calls=%fused_computation.41 | convolution fusion | flops 70778864 | bytes 5382208 | tf_op jit(solution)/shard_map/bc,kca->kba/dot_general | solution.py:37
  119.5 11.8 %psum.21 = f32[16]{0:T(128)S(1)} all-reduce(f32[16]{0:T(128)S(1)} %get-tuple-element.133), channel_id=1, replica_groups=mesh['blk'=8,'vec'=4] {'blk'}, use_global_device_ids=true, to_apply=%region_12.13 | all-reduce | flops 16 | bytes 128 | tf_op jit(solution)/shard_map/psum | solution.py:54
  131.2 0.0 copy-done.3
  131.2 3.9 %multiply_reduce_fusion.1 = (f32[16]{0:T(128)S(1)}, f32[16,64,512]{2,1,0:T(8,128)}) fusion(f32[64,512]{1,0:T(8,128)S(1)} %copy-done.6, f32[16,64,512]{2,1,0:T(8,128)} %get-tuple-element.134, bf16[16,64,512]{2,1,0:T(8,128)(2,1)S(1)} %copy-done.3, f32[16]{0:T(128)S(1)} %psum.21), kind=kLoop, calls=%fused_computation.44 | loop fusion | flops 5242864 | bytes 5374080 | tf_op jit(solution)/shard_map/reduce_sum | solution.py:58
  135.2 5.9 %fusion.32 = f32[64,16]{0,1:T(8,128)S(1)} fusion(f32[16,64,512]{2,1,0:T(8,128)S(1)} %copy-done.4, bf16[128,64,512]{2,0,1:T(8,128)(2,1)} %constant_dynamic-update-slice_fusion, s32[]{:T(128)S(6)} %select_n.32), kind=kOutput, calls=%fused_computation.46 | convolution fusion | flops 402653184 | bytes 6295556 | tf_op jit(solution)/shard_map/kba,lba->kl/dot_general | solution.py:49
  141.0 12.9 %all-reduce = (f32[16]{0:T(128)S(1)}, f32[64,16]{0,1:T(8,128)}) all-reduce(f32[16]{0:T(128)S(1)} %get-tuple-element.125, f32[64,16]{0,1:T(8,128)S(1)} %fusion.32), channel_id=1, replica_groups=mesh['blk'=8,'vec'=4] {'blk'}, use_global_device_ids=true, to_apply=%region_14.15 | all-reduce | flops 1040 | bytes 8320 | tf_op jit(solution)/shard_map/psum | solution.py:58
  153.9 0.0 copy-done.5
  153.9 1.3 multiply_convert_fusion
  (9 shorter events, 0.0 us)
Async XLA Ops:
  7.2 108.1 %copy-start = (bf16[512,512]{1,0:T(8,128)(2,1)S(1)}, bf16[512,512]{1,0:T(8,128)(2,1)}, u32[]{:S(2)}) copy-start(bf16[512,512]{1,0:T(8,128)(2,1)} %param.23) | copy-start | bytes 1572868
  7.2 57.0 %copy-start.7 = (s32[1,6]{1,0:T(1,128)S(1)}, s32[1,6]{1,0:T(1,128)}, u32[]{:S(2)}) copy-start(s32[1,6]{1,0:T(1,128)} %param.21) | copy-start | bytes 76
  7.2 94.5 %all-gather.2.cloned.1.call-start = ((), (), s32[]{:S(2)}) async-start(), calls=%async_computation | async-start | bytes 9437184 | tf_op jit(solution)/shard_map/all_gather | solution.py:18
  9.7 28.3 %collective-permute-start = (bf16[16,64,512]{2,0,1:T(8,128)(2,1)S(1)}, bf16[16,64,512]{2,0,1:T(8,128)(2,1)S(1)}, u32[]{:S(2)}, u32[]{:S(2)}) collective-permute-start(bf16[16,64,512]{2,0,1:T(8,128)(2,1)S(1)} %copy.9), channel_id=1, source_target_pairs={{0,1},{1,2},{2,3},{3,0},{4,5},{5,6},{6,7},{7,4},{8,9},{9,10},{10,1... | collective-permute-start | bytes 3145736 | tf_op jit(solution)/shard_map/ppermute | solution.py:45
  38.0 26.1 %collective-permute-start.1 = (bf16[16,64,512]{2,0,1:T(8,128)(2,1)S(1)}, bf16[16,64,512]{2,0,1:T(8,128)(2,1)S(1)}, u32[]{:S(2)}, u32[]{:S(2)}) collective-permute-start(bf16[16,64,512]{2,0,1:T(8,128)(2,1)S(1)} %collective-permute-done), channel_id=1, source_target_pairs={{0,1},{1,2},{2,3},{3,0},{4,5},{5,6},{6,7},{7,4},{8,9},{9,10},{10,1... | collective-permute-start | bytes 3145736 | tf_op jit(solution)/shard_map/ppermute | solution.py:45
  64.1 25.4 %collective-permute-start.2 = (bf16[16,64,512]{2,0,1:T(8,128)(2,1)S(1)}, bf16[16,64,512]{2,0,1:T(8,128)(2,1)}, u32[]{:S(2)}, u32[]{:S(2)}) collective-permute-start(bf16[16,64,512]{2,0,1:T(8,128)(2,1)S(1)} %collective-permute-done.1), channel_id=1, source_target_pairs={{0,1},{1,2},{2,3},{3,0},{4,5},{5,6},{6,7},{7,4},{8,9},{9,10},{10,1... | collective-permute-start | bytes 3145736 | tf_op jit(solution)/shard_map/ppermute | solution.py:45
  91.8 2.2 %copy-start.1 = (bf16[16,64,512]{2,1,0:T(8,128)(2,1)S(1)}, bf16[16,64,512]{2,1,0:T(8,128)(2,1)}, u32[]{:S(2)}) copy-start(bf16[16,64,512]{2,1,0:T(8,128)(2,1)} %param.19) | copy-start | bytes 3145732
  115.3 2.1 %copy-start.2 = (bf16[16,64,512]{2,1,0:T(8,128)(2,1)S(1)}, bf16[16,64,512]{2,1,0:T(8,128)(2,1)}, u32[]{:S(2)}) copy-start(bf16[16,64,512]{2,1,0:T(8,128)(2,1)} %param.19) | copy-start | bytes 3145732
  115.3 2.1 %copy-start.6 = (f32[64,512]{1,0:T(8,128)S(1)}, f32[64,512]{1,0:T(8,128)}, u32[]{:S(2)}) copy-start(f32[64,512]{1,0:T(8,128)} %param.25) | copy-start | bytes 393220
  115.3 2.1 %copy-start.8 = (bf16[64,64]{1,0:T(8,128)(2,1)S(1)}, bf16[64,64]{1,0:T(8,128)(2,1)}, u32[]{:S(2)}) copy-start(bf16[64,64]{1,0:T(8,128)(2,1)} %param.24) | copy-start | bytes 24580
  117.4 13.8 %copy-start.3 = (bf16[16,64,512]{2,1,0:T(8,128)(2,1)S(1)}, bf16[16,64,512]{2,1,0:T(8,128)(2,1)}, u32[]{:S(2)}) copy-start(bf16[16,64,512]{2,1,0:T(8,128)(2,1)} %param.19) | copy-start | bytes 3145732
  131.2 3.9 %copy-start.4 = (f32[16,64,512]{2,1,0:T(8,128)S(1)}, f32[16,64,512]{2,1,0:T(8,128)}, u32[]{:S(2)}) copy-start(f32[16,64,512]{2,1,0:T(8,128)} %get-tuple-element.134) | copy-start | bytes 6291460
  135.2 18.7 %copy-start.5 = (f32[16,64,512]{2,1,0:T(8,128)S(1)}, f32[16,64,512]{2,1,0:T(8,128)}, u32[]{:S(2)}) copy-start(f32[16,64,512]{2,1,0:T(8,128)} %get-tuple-element.126) | copy-start | bytes 6291460
Sparse Core Ops, SparseCore 0:
  9.9 58.5 all-gather.1
